TPU v7x, 32 devices: a whole 2x2x4 slice. The times are simulated.
32 devices in a mesh: batch: 2 (over x), row: 4 (over z), col: 4 (over y, core).
Axes of the slice: x: 2, y: 2, z: 4, core: 2. Of those that a mesh axis runs over, the one named last changes fastest.
Arguments:
- left_op: bfloat16 [24576, 12288], P(('batch', 'row'), 'col'), parts along dimension 0
- left_start: float32 [24576, 128], P(('batch', 'row', 'col')), parts along dimension 0
- right_op: bfloat16 [24576, 12288], P(('batch', 'row'), 'col'), parts along dimension 0
- right_start: float32 [24576, 128], P(('batch', 'row', 'col')), parts along dimension 0
Outputs:
- output 1: float32 [24576, 128], P(('batch', 'row', 'col')), parts along dimension 0
- output 2: float32 [256, 128], P('batch'), parts along dimension 0
- output 3: float32 [24576, 128], P(('batch', 'row', 'col')), parts along dimension 0
- output 4: float32 [256, 128], P('batch'), parts along dimension 0
There are 2 independent parts. A program takes and returns all parts, laid end to end along the dimension named above; each array names one.
All inputs are finite; a program needn't handle non-finite values.
Results may differ from a plain program's by a relative error of at most 0.001.
Values are sent between devices in bfloat16 or wider.
A program may use at most 1 GiB of HBM per device.

v0:
```python
import jax
import jax.numpy as jnp
from jax import lax
from jax.sharding import PartitionSpec as P

SWEEPS = 4
ROW_CONTRACT = (((0,), (0,)), ((), ()))


def gram_total(lhs_mat, rhs_mat, precision, grid_axes):
    local_gram = lax.dot_general(lhs_mat, rhs_mat, ROW_CONTRACT, precision=precision, preferred_element_type=jnp.float32)
    return lax.psum(local_gram, grid_axes)


def cholqr_step(y_mat, gram_mat):
    chol_low = jnp.linalg.cholesky(gram_mat)
    return lax.linalg.triangular_solve(chol_low, y_mat, left_side=False, lower=True, transpose_a=True)


def orthonormalize(y_sub, total_rows, grid_axes):
    y_half = y_sub.astype(jnp.bfloat16)
    gram_one = gram_total(y_half, y_half, None, grid_axes) / total_rows
    y_one = cholqr_step(y_sub, gram_one)
    gram_two = gram_total(y_one, y_one, lax.Precision.HIGHEST, grid_axes) / total_rows
    return cholqr_step(y_one, gram_two)


def solution(mesh):
    row_size = mesh.shape["row"]
    col_size = mesh.shape["col"]
    grid_axes = ("row", "col")
    perm_pairs = [(src_index, (src_index % row_size) * col_size + src_index // row_size) for src_index in range(row_size * col_size)]

    def apply_op(op_blk, x_sub):
        x_moved = lax.ppermute(x_sub.astype(jnp.bfloat16), grid_axes, perm_pairs)
        x_col = lax.all_gather(x_moved, "row", axis=0, tiled=True)
        partial_prod = jnp.dot(op_blk, x_col, preferred_element_type=jnp.float32)
        return lax.psum_scatter(partial_prod, "col", scatter_dimension=0, tiled=True)

    def iterate_local(op_blk, start_sub):
        total_rows = op_blk.shape[0] * row_size
        x_sub = start_sub
        for sweep_index in range(SWEEPS):
            x_sub = orthonormalize(apply_op(op_blk, x_sub), total_rows, grid_axes)
        z_sub = apply_op(op_blk, x_sub)
        rayleigh = gram_total(x_sub, z_sub, lax.Precision.HIGHEST, grid_axes) / total_rows
        return x_sub, rayleigh

    def local_program(left_op, left_start, right_op, right_start):
        left_basis, left_rayleigh = iterate_local(left_op, left_start)
        right_basis, right_rayleigh = iterate_local(right_op, right_start)
        return left_basis, left_rayleigh, right_basis, right_rayleigh

    op_spec = P(("batch", "row"), "col")
    vec_spec = P(("batch", "row", "col"), None)
    small_spec = P("batch", None)
    return jax.shard_map(local_program, mesh=mesh, in_specs=(op_spec, vec_spec, op_spec, vec_spec), out_specs=(vec_spec, small_spec, vec_spec, small_spec), check_vma=False)
```

profile of v0, /device:TPU:0, one launch (start us, length us, event | category | flops | bytes accessed | tf_op | source)
XLA Modules:
  0.0 1835.7 jit_solution(15451908430008546030)
XLA Ops:
  9.0 31.4 %all_gather.35 = bf16[3072,128]{1,0:T(8,128)(2,1)S(1)} all-gather(bf16[768,128]{1,0:T(8,128)(2,1)S(1)} %collective-permute-done.5), channel_id=1, replica_groups=mesh['batch'=2,'row'=4,'col'=4] {'row'}, dimensions={0}, use_global_device_ids=true | all-gather | bytes 983040 | tf_op jit(solution)/shard_map/all_gather | solution.py:36
  51.3 28.9 %all_gather.30 = bf16[3072,128]{1,0:T(8,128)(2,1)S(1)} all-gather(bf16[768,128]{1,0:T(8,128)(2,1)S(1)} %collective-permute-done), channel_id=1, replica_groups=mesh['batch'=2,'row'=4,'col'=4] {'row'}, dimensions={0}, use_global_device_ids=true | all-gather | bytes 983040 | tf_op jit(solution)/shard_map/all_gather | solution.py:36
  92.4 27.4 %reduce-scatter.11.cloned.1.call-done = f32[768,128]{1,0:T(8,128)} async-done(((f32[3072,128]{1,0:T(8,128)}), f32[768,128]{1,0:T(8,128)}) %reduce-scatter.11.cloned.1.call-update) | async-done | bytes 393232 | tf_op jit(solution)/shard_map/reduce_scatter | solution.py:38
  122.1 92.8 %all-reduce.35.cloned.1.call-done = (f32[128,128]{0,1:T(8,128)}, f32[128,128]{0,1:T(8,128)}) async-done(((f32[128,128]{0,1:T(8,128)}, f32[128,128]{0,1:T(8,128)}), (f32[128,128]{0,1:T(8,128)}, f32[128,128]{0,1:T(8,128)})) %all-reduce.35.cloned.1.call-update) | async-done | bytes 131088 | tf_op jit(solution)/shard_map/psum | solution.py:12
  217.7 11.7 cholesky.342
  243.2 11.7 cholesky.254
  269.2 90.1 %all-reduce.33.cloned.1.call-done = (f32[128,128]{0,1:T(8,128)}, f32[128,128]{0,1:T(8,128)}) async-done(((f32[128,128]{0,1:T(8,128)}, f32[128,128]{0,1:T(8,128)}), (f32[128,128]{0,1:T(8,128)}, f32[128,128]{0,1:T(8,128)})) %all-reduce.33.cloned.1.call-update) | async-done | bytes 131088 | tf_op jit(solution)/shard_map/psum | solution.py:12
  361.1 11.7 cholesky.353
  385.2 29.4 %all_gather.36 = bf16[3072,128]{0,1:T(8,128)(2,1)S(1)} all-gather(bf16[768,128]{0,1:T(8,128)(2,1)S(1)} %collective-permute-done.6), channel_id=1, replica_groups=mesh['batch'=2,'row'=4,'col'=4] {'row'}, dimensions={0}, use_global_device_ids=true | all-gather | bytes 983040 | tf_op jit(solution)/shard_map/all_gather | solution.py:36
  414.6 13.8 convolution_bitcast_fusion.3
  428.6 11.7 cholesky.265
  452.7 26.9 %all_gather.31 = bf16[3072,128]{0,1:T(8,128)(2,1)S(1)} all-gather(bf16[768,128]{0,1:T(8,128)(2,1)S(1)} %collective-permute-done.1), channel_id=1, replica_groups=mesh['batch'=2,'row'=4,'col'=4] {'row'}, dimensions={0}, use_global_device_ids=true | all-gather | bytes 983040 | tf_op jit(solution)/shard_map/all_gather | solution.py:36
  479.6 13.8 convolution_bitcast_fusion.7
  495.5 26.5 %reduce-scatter.13.cloned.1.call-done = f32[768,128]{0,1:T(8,128)} async-done(((f32[3072,128]{0,1:T(8,128)}), f32[768,128]{0,1:T(8,128)}) %reduce-scatter.13.cloned.1.call-update) | async-done | bytes 393232 | tf_op jit(solution)/shard_map/reduce_scatter | solution.py:38
  524.4 92.7 %all-reduce.31.cloned.1.call-done = (f32[128,128]{0,1:T(8,128)}, f32[128,128]{0,1:T(8,128)}) async-done(((f32[128,128]{0,1:T(8,128)}, f32[128,128]{0,1:T(8,128)}), (f32[128,128]{0,1:T(8,128)}, f32[128,128]{0,1:T(8,128)})) %all-reduce.31.cloned.1.call-update) | async-done | bytes 131088 | tf_op jit(solution)/shard_map/psum | solution.py:12
  618.9 11.7 cholesky.364
  646.2 11.7 cholesky.276
  671.9 90.1 %all-reduce.29.cloned.1.call-done = (f32[128,128]{0,1:T(8,128)}, f32[128,128]{0,1:T(8,128)}) async-done(((f32[128,128]{0,1:T(8,128)}, f32[128,128]{0,1:T(8,128)}), (f32[128,128]{0,1:T(8,128)}, f32[128,128]{0,1:T(8,128)})) %all-reduce.29.cloned.1.call-update) | async-done | bytes 131088 | tf_op jit(solution)/shard_map/psum | solution.py:12
  763.8 11.7 cholesky.375
  787.9 29.7 %all_gather.37 = bf16[3072,128]{0,1:T(8,128)(2,1)S(1)} all-gather(bf16[768,128]{0,1:T(8,128)(2,1)S(1)} %collective-permute-done.7), channel_id=1, replica_groups=mesh['batch'=2,'row'=4,'col'=4] {'row'}, dimensions={0}, use_global_device_ids=true | all-gather | bytes 983040 | tf_op jit(solution)/shard_map/all_gather | solution.py:36
  817.6 13.8 convolution_bitcast_fusion.2
  831.6 11.7 cholesky.287
  855.7 26.9 %all_gather.32 = bf16[3072,128]{0,1:T(8,128)(2,1)S(1)} all-gather(bf16[768,128]{0,1:T(8,128)(2,1)S(1)} %collective-permute-done.2), channel_id=1, replica_groups=mesh['batch'=2,'row'=4,'col'=4] {'row'}, dimensions={0}, use_global_device_ids=true | all-gather | bytes 983040 | tf_op jit(solution)/shard_map/all_gather | solution.py:36
  882.6 13.8 convolution_bitcast_fusion.6
  898.5 26.5 %reduce-scatter.15.cloned.1.call-done = f32[768,128]{0,1:T(8,128)} async-done(((f32[3072,128]{0,1:T(8,128)}), f32[768,128]{0,1:T(8,128)}) %reduce-scatter.15.cloned.1.call-update) | async-done | bytes 393232 | tf_op jit(solution)/shard_map/reduce_scatter | solution.py:38
  927.1 92.9 %all-reduce.27.cloned.1.call-done = (f32[128,128]{0,1:T(8,128)}, f32[128,128]{0,1:T(8,128)}) async-done(((f32[128,128]{0,1:T(8,128)}, f32[128,128]{0,1:T(8,128)}), (f32[128,128]{0,1:T(8,128)}, f32[128,128]{0,1:T(8,128)})) %all-reduce.27.cloned.1.call-update) | async-done | bytes 131088 | tf_op jit(solution)/shard_map/psum | solution.py:12
  1021.8 11.7 cholesky.386
  1049.1 11.7 cholesky.298
  1075.1 90.1 %all-reduce.25.cloned.1.call-done = (f32[128,128]{0,1:T(8,128)}, f32[128,128]{0,1:T(8,128)}) async-done(((f32[128,128]{0,1:T(8,128)}, f32[128,128]{0,1:T(8,128)}), (f32[128,128]{0,1:T(8,128)}, f32[128,128]{0,1:T(8,128)})) %all-reduce.25.cloned.1.call-update) | async-done | bytes 131088 | tf_op jit(solution)/shard_map/psum | solution.py:12
  1167.0 11.7 cholesky.397
  1191.1 29.4 %all_gather.38 = bf16[3072,128]{0,1:T(8,128)(2,1)S(1)} all-gather(bf16[768,128]{0,1:T(8,128)(2,1)S(1)} %collective-permute-done.8), channel_id=1, replica_groups=mesh['batch'=2,'row'=4,'col'=4] {'row'}, dimensions={0}, use_global_device_ids=true | all-gather | bytes 983040 | tf_op jit(solution)/shard_map/all_gather | solution.py:36
  1220.5 13.8 convolution_bitcast_fusion.1
  1234.6 11.7 cholesky.309
  1258.7 26.9 %all_gather.33 = bf16[3072,128]{0,1:T(8,128)(2,1)S(1)} all-gather(bf16[768,128]{0,1:T(8,128)(2,1)S(1)} %collective-permute-done.3), channel_id=1, replica_groups=mesh['batch'=2,'row'=4,'col'=4] {'row'}, dimensions={0}, use_global_device_ids=true | all-gather | bytes 983040 | tf_op jit(solution)/shard_map/all_gather | solution.py:36
  1285.5 13.8 convolution_bitcast_fusion.5
  1301.4 26.4 %reduce-scatter.17.cloned.1.call-done = f32[768,128]{0,1:T(8,128)} async-done(((f32[3072,128]{0,1:T(8,128)}), f32[768,128]{0,1:T(8,128)}) %reduce-scatter.17.cloned.1.call-update) | async-done | bytes 393232 | tf_op jit(solution)/shard_map/reduce_scatter | solution.py:38
  1330.3 92.5 %all-reduce.23.cloned.1.call-done = (f32[128,128]{0,1:T(8,128)}, f32[128,128]{0,1:T(8,128)}) async-done(((f32[128,128]{0,1:T(8,128)}, f32[128,128]{0,1:T(8,128)}), (f32[128,128]{0,1:T(8,128)}, f32[128,128]{0,1:T(8,128)})) %all-reduce.23.cloned.1.call-update) | async-done | bytes 131088 | tf_op jit(solution)/shard_map/psum | solution.py:12
  1424.5 11.7 cholesky.408
  1451.9 11.7 cholesky.320
  1477.6 90.1 %all-reduce.21.cloned.1.call-done = (f32[128,128]{0,1:T(8,128)}, f32[128,128]{0,1:T(8,128)}) async-done(((f32[128,128]{0,1:T(8,128)}, f32[128,128]{0,1:T(8,128)}), (f32[128,128]{0,1:T(8,128)}, f32[128,128]{0,1:T(8,128)})) %all-reduce.21.cloned.1.call-update) | async-done | bytes 131088 | tf_op jit(solution)/shard_map/psum | solution.py:12
  1569.5 11.7 cholesky.419
  1593.6 29.5 %all_gather.39 = bf16[3072,128]{0,1:T(8,128)(2,1)S(1)} all-gather(bf16[768,128]{0,1:T(8,128)(2,1)S(1)} %collective-permute-done.9), channel_id=1, replica_groups=mesh['batch'=2,'row'=4,'col'=4] {'row'}, dimensions={0}, use_global_device_ids=true | all-gather | bytes 983040 | tf_op jit(solution)/shard_map/all_gather | solution.py:36
  1623.0 13.8 convolution_bitcast_fusion
  1637.1 11.7 cholesky.331
  1661.2 27.1 %all_gather.34 = bf16[3072,128]{0,1:T(8,128)(2,1)S(1)} all-gather(bf16[768,128]{0,1:T(8,128)(2,1)S(1)} %collective-permute-done.4), channel_id=1, replica_groups=mesh['batch'=2,'row'=4,'col'=4] {'row'}, dimensions={0}, use_global_device_ids=true | all-gather | bytes 983040 | tf_op jit(solution)/shard_map/all_gather | solution.py:36
  1688.3 13.8 convolution_bitcast_fusion.4
  1704.3 26.3 %reduce-scatter.19.cloned.1.call-done = f32[768,128]{0,1:T(8,128)} async-done(((f32[3072,128]{0,1:T(8,128)}), f32[768,128]{0,1:T(8,128)}) %reduce-scatter.19.cloned.1.call-update) | async-done | bytes 393232 | tf_op jit(solution)/shard_map/reduce_scatter | solution.py:38
  1734.6 91.1 %all-reduce.19.cloned.1.call-done = (f32[128,128]{0,1:T(8,128)}, f32[128,128]{0,1:T(8,128)}) async-done(((f32[128,128]{0,1:T(8,128)}, f32[128,128]{0,1:T(8,128)}), (f32[128,128]{0,1:T(8,128)}, f32[128,128]{0,1:T(8,128)})) %all-reduce.19.cloned.1.call-update) | async-done | bytes 131088 | tf_op jit(solution)/shard_map/psum | solution.py:12
  (228 shorter events, 281.2 us)
Async XLA Ops:
  7.2 43.4 %copy-start = (f32[768,128]{1,0:T(8,128)S(1)}, f32[768,128]{1,0:T(8,128)}, u32[]{:S(2)}) copy-start(f32[768,128]{1,0:T(8,128)} %param.8) | copy-start | bytes 1179652
  7.2 83.2 %reduce-scatter.21.cloned.1.call-start = ((), (), s32[]{:S(2)}) async-start(), calls=%async_computation.15 | async-start | bytes 1966080 | tf_op jit(solution)/shard_map/reduce_scatter | solution.py:38
  8.3 0.7 collective-permute-start.5
  50.5 69.4 %reduce-scatter.11.cloned.1.call-start = ((), (), s32[]{:S(2)}) async-start(), calls=%async_computation.10 | async-start | bytes 1966080 | tf_op jit(solution)/shard_map/reduce_scatter | solution.py:38
  50.6 0.7 collective-permute-start
  90.3 124.6 %all-reduce.35.cloned.1.call-start = ((), (), s32[]{:S(2)}) async-start(), calls=%async_computation.28 | async-start | bytes 262144 | tf_op jit(solution)/shard_map/psum | solution.py:12
  121.9 237.4 %all-reduce.33.cloned.1.call-start = ((), (), s32[]{:S(2)}) async-start(), calls=%async_computation.27 | async-start | bytes 262144 | tf_op jit(solution)/shard_map/psum | solution.py:12
  269.1 224.4 %reduce-scatter.23.cloned.1.call-start = ((), (), s32[]{:S(2)}) async-start(), calls=%async_computation.16 | async-start | bytes 1966080 | tf_op jit(solution)/shard_map/reduce_scatter | solution.py:38
  359.3 69.3 %copy-start.2 = (f32[128,128]{0,1:T(8,128)S(1)}, f32[128,128]{0,1:T(8,128)}, u32[]{:S(2)}) copy-start(f32[128,128]{0,1:T(8,128)} %get-tuple-element.24) | copy-start | bytes 196612
  384.5 0.7 collective-permute-start.6
  428.5 93.5 %reduce-scatter.13.cloned.1.call-start = ((), (), s32[]{:S(2)}) async-start(), calls=%async_computation.11 | async-start | bytes 1966080 | tf_op jit(solution)/shard_map/reduce_scatter | solution.py:38
  452.0 0.7 collective-permute-start.1
  493.4 123.6 %all-reduce.31.cloned.1.call-start = ((), (), s32[]{:S(2)}) async-start(), calls=%async_computation.26 | async-start | bytes 262144 | tf_op jit(solution)/shard_map/psum | solution.py:12
  523.9 238.0 %all-reduce.29.cloned.1.call-start = ((), (), s32[]{:S(2)}) async-start(), calls=%async_computation.25 | async-start | bytes 262144 | tf_op jit(solution)/shard_map/psum | solution.py:12
  671.9 224.6 %reduce-scatter.25.cloned.1.call-start = ((), (), s32[]{:S(2)}) async-start(), calls=%async_computation.17 | async-start | bytes 1966080 | tf_op jit(solution)/shard_map/reduce_scatter | solution.py:38
  762.0 69.5 %copy-start.3 = (f32[128,128]{0,1:T(8,128)S(1)}, f32[128,128]{0,1:T(8,128)}, u32[]{:S(2)}) copy-start(f32[128,128]{0,1:T(8,128)} %get-tuple-element.20) | copy-start | bytes 196612
  787.2 0.7 collective-permute-start.7
  831.4 93.5 %reduce-scatter.15.cloned.1.call-start = ((), (), s32[]{:S(2)}) async-start(), calls=%async_computation.12 | async-start | bytes 1966080 | tf_op jit(solution)/shard_map/reduce_scatter | solution.py:38
  855.0 0.7 collective-permute-start.2
  896.4 123.6 %all-reduce.27.cloned.1.call-start = ((), (), s32[]{:S(2)}) async-start(), calls=%async_computation.24 | async-start | bytes 262144 | tf_op jit(solution)/shard_map/psum | solution.py:12
  926.9 238.3 %all-reduce.25.cloned.1.call-start = ((), (), s32[]{:S(2)}) async-start(), calls=%async_computation.23 | async-start | bytes 262144 | tf_op jit(solution)/shard_map/psum | solution.py:12
  1075.0 224.4 %reduce-scatter.27.cloned.1.call-start = ((), (), s32[]{:S(2)}) async-start(), calls=%async_computation.18 | async-start | bytes 1966080 | tf_op jit(solution)/shard_map/reduce_scatter | solution.py:38
  1165.2 69.3 %copy-start.4 = (f32[128,128]{0,1:T(8,128)S(1)}, f32[128,128]{0,1:T(8,128)}, u32[]{:S(2)}) copy-start(f32[128,128]{0,1:T(8,128)} %get-tuple-element.16) | copy-start | bytes 196612
  1190.4 0.7 collective-permute-start.8
  1234.4 93.4 %reduce-scatter.17.cloned.1.call-start = ((), (), s32[]{:S(2)}) async-start(), calls=%async_computation.13 | async-start | bytes 1966080 | tf_op jit(solution)/shard_map/reduce_scatter | solution.py:38
  1258.0 0.7 collective-permute-start.3
  1299.4 123.4 %all-reduce.23.cloned.1.call-start = ((), (), s32[]{:S(2)}) async-start(), calls=%async_computation.22 | async-start | bytes 262144 | tf_op jit(solution)/shard_map/psum | solution.py:12
  1329.8 237.9 %all-reduce.21.cloned.1.call-start = ((), (), s32[]{:S(2)}) async-start(), calls=%async_computation.21 | async-start | bytes 262144 | tf_op jit(solution)/shard_map/psum | solution.py:12
  1477.5 224.7 %reduce-scatter.29.cloned.1.call-start = ((), (), s32[]{:S(2)}) async-start(), calls=%async_computation.19 | async-start | bytes 1966080 | tf_op jit(solution)/shard_map/reduce_scatter | solution.py:38
  1567.7 69.3 %copy-start.1 = (f32[128,128]{0,1:T(8,128)S(1)}, f32[128,128]{0,1:T(8,128)}, u32[]{:S(2)}) copy-start(f32[128,128]{0,1:T(8,128)} %get-tuple-element.12) | copy-start | bytes 196612
  1592.9 0.7 collective-permute-start.9
  1636.9 93.8 %reduce-scatter.19.cloned.1.call-start = ((), (), s32[]{:S(2)}) async-start(), calls=%async_computation.14 | async-start | bytes 1966080 | tf_op jit(solution)/shard_map/reduce_scatter | solution.py:38
  1660.5 0.7 collective-permute-start.4
  1702.1 123.6 %all-reduce.19.cloned.1.call-start = ((), (), s32[]{:S(2)}) async-start(), calls=%async_computation.20 | async-start | bytes 262144 | tf_op jit(solution)/shard_map/psum | solution.py:12
Sparse Core Ops, SparseCore 0:
  50.6 29.0 reduce-scatter.20
  90.5 29.3 reduce-scatter.10
  124.0 90.9 all-reduce.34
  269.3 89.9 all-reduce.32
  428.6 26.5 reduce-scatter.22
  493.6 28.3 reduce-scatter.12
  526.1 90.9 all-reduce.30
  672.0 89.9 all-reduce.28
  831.5 26.4 reduce-scatter.24
  896.5 28.3 reduce-scatter.14
  929.0 90.9 all-reduce.26
  1075.1 89.9 all-reduce.24
  1234.5 26.4 reduce-scatter.26
  1299.5 28.2 reduce-scatter.16
  1331.8 90.9 all-reduce.22
  1477.7 89.9 all-reduce.20
  1637.0 26.4 reduce-scatter.28
  1702.3 28.3 reduce-scatter.18
  1734.8 90.9 all-reduce.18
where the time goes:
time: 1840 us
  waiting for transfers between devices  956 us (52%)
  other arithmetic  389 us (21%)
  blocking collectives  286 us (16%)
  matrix products  176 us (10%)
    psum x9, waiting for transfers between devices, gram_total(): return lax.psum(local_gram, grid_axes)  822 us
    all_gather x10, blocking collectives, apply_op(): x_col = lax.all_gather(x_moved, 'row', axis=0, tiled=True)  286 us
    another operation x48, other arithmetic, cholqr_step(): chol_low = jnp.linalg.cholesky(gram_mat)  198 us
    another operation x32, other arithmetic, cholqr_step(): lax.linalg.triangular_solve(chol_low, y_mat, left_side=False, lower=True,...  168 us
    reduce_scatter x10, waiting for transfers between devices, apply_op(): lax.psum_scatter(partial_prod, 'col', scatter_dimension=0, tiled=True)  133 us
    dot_general x10, matrix products, apply_op(): partial_prod = jnp.dot(op_blk, x_col, preferred_element_type=jnp.float32)  131 us
  transfers between devices with their start and end apart: 29, of which 14 were waited for; matrix products, arithmetic and copies ran while one was open for 9% of the time, Pallas kernels for 0%

commit v1 on v0

v1 whole, which is shorter than its diff:
```python
import functools

import jax
import jax.numpy as jnp
from jax import lax
from jax.experimental import pallas as pl
from jax.experimental.pallas import tpu as pltpu
from jax.sharding import PartitionSpec as P

SWEEPS = 4
CHUNKS = 2
MESH = pl.DeviceIdType.MESH
HIGHEST = lax.Precision.HIGHEST
OPS = (0, 1)
F32 = jnp.float32
BF16 = jnp.bfloat16


def dot(lhs, rhs, lhs_dim, rhs_dim, precision=None):
    dims = (((lhs_dim,), (rhs_dim,)), ((), ()))
    return lax.dot_general(lhs, rhs, dims, precision=precision, preferred_element_type=F32)


def split3(v):
    one = v.astype(BF16).astype(F32)
    rest = v - one
    two = rest.astype(BF16).astype(F32)
    return one, two, rest - two


def kernel(rows, col, left_op, left_start, right_op, right_start, left_basis, left_ray, right_basis, right_ray,
           a_v, xg, xz, xf, part, rsa, sb, rsb, yv, gp, g1, s1, g2, slots, gs, gw, mv,
           load_sem, rsa_ss, rsa_rs, rsb_ss, rsb_rs, g1_ss, g1_rs, g2_ss, g2_rs, sl_ss, sl_rs, g4_ss, g4_rs,
           zr_ss, zl_ss, z_rs, p_ss, p_rs):
    b, z, c = lax.axis_index("batch"), lax.axis_index("row"), lax.axis_index("col")
    y, k = c // 2, c % 2
    blk = a_v.shape[1]
    sub = blk // col
    piece = sub // CHUNKS
    total = blk * rows
    half, quarter = 64, 32

    def dev(zz, yy, kk):
        return (b, zz, 2 * yy + kk)

    def rcopy(src, dst, ss, rs, to):
        return pltpu.make_async_remote_copy(src_ref=src, dst_ref=dst, send_sem=ss, recv_sem=rs, device_id=to, device_id_type=MESH)

    partner, across = dev(z, y, 1 - k), dev(z, 1 - y, k)

    def load(op, j):
        src = (left_op, right_op)[op]
        rng = pl.ds(j * sub, sub)
        return pltpu.make_async_copy(src.at[rng], a_v.at[op, rng], load_sem.at[op, j])

    for op in OPS:
        for j in range(col):
            load(op, j).start()

    barrier = pltpu.get_barrier_semaphore()
    me = z * col + c
    count = rows * col
    for d in range(1, count):
        peer = lax.rem(me + d, count)
        pl.semaphore_signal(barrier, inc=1, device_id=(b, peer // col, lax.rem(peer, col)), device_id_type=MESH)
    pl.semaphore_wait(barrier, count - 1)

    def z_copy(op, slot, h, step):
        rng = pl.ds(h * piece, piece)
        to, ss = (dev(z + 1, y, k), zr_ss) if step > 0 else (dev(z - 1, y, k), zl_ss)
        return rcopy(xz.at[op, slot, rng], xz.at[op, slot, rng], ss.at[op, slot, h], z_rs.at[op, slot, h], to)

    def p_copy(op, slot, h):
        src = xz.at[op, slot, pl.ds(h * piece, piece)]
        dst = xg.at[op, pl.ds(c * sub + h * piece, piece)]
        return rcopy(src, dst, p_ss.at[op, slot, h], p_rs.at[op, c, h], dev(z, slot // 2, lax.rem(slot, 2)))

    def p_local(op, slot, h):
        src = xz.at[op, slot, pl.ds(h * piece, piece)]
        dst = xg.at[op, pl.ds(c * sub + h * piece, piece)]
        return pltpu.make_async_copy(src, dst, p_rs.at[op, c, h])

    def p_start(op, slot, h):
        @pl.when(slot == c)
        def _():
            p_local(op, slot, h).start()

        @pl.when(slot != c)
        def _():
            p_copy(op, slot, h).start()

    def spread_begin(op):
        for h in range(CHUNKS):
            @pl.when(z < rows - 1)
            def _():
                z_copy(op, z, h, 1).start()

            @pl.when(z > 0)
            def _():
                z_copy(op, z, h, -1).start()
        for h in range(CHUNKS):
            p_start(op, z, h)

    def spread_step(op, t):
        for h in range(CHUNKS):
            @pl.when(z - t >= 0)
            def _():
                slot = z - t
                z_copy(op, slot, h, 1).wait_recv()

                @pl.when(z < rows - 1)
                def _():
                    z_copy(op, slot, h, 1).start()

                p_start(op, slot, h)

            @pl.when(z + t < rows)
            def _():
                slot = z + t
                z_copy(op, slot, h, -1).wait_recv()

                @pl.when(z > 0)
                def _():
                    z_copy(op, slot, h, -1).start()

                p_start(op, slot, h)

    def spread_end(op):
        for src in range(col):
            for h in range(CHUNKS):
                dst = xg.at[op, pl.ds(src * sub + h * piece, piece)]
                pltpu.make_async_copy(dst, dst, p_rs.at[op, src, h]).wait()

    def spread_sent(op):
        for slot in range(rows):
            for h in range(CHUNKS):
                @pl.when((slot <= z) & (z < rows - 1))
                def _():
                    z_copy(op, slot, h, 1).wait_send()

                @pl.when((slot >= z) & (z > 0))
                def _():
                    z_copy(op, slot, h, -1).wait_send()

                @pl.when(slot != c)
                def _():
                    p_copy(op, slot, h).wait_send()

    def core_copy(op, yy):
        return rcopy(part.at[op, 2 * yy + 1 - k], rsa.at[op, yy], rsa_ss.at[op, yy], rsa_rs.at[op, yy], partner)

    def y_copy(op):
        return rcopy(sb.at[op], rsb.at[op], rsb_ss.at[op], rsb_rs.at[op], across)

    def product(op):
        def step(i, carry):
            yy = (1 - y) + (i // 2) * (2 * y - 1)
            kk = (1 - k) + lax.rem(i, 2) * (2 * k - 1)
            j = 2 * yy + kk
            part[op, j] = dot(a_v[op, pl.ds(pl.multiple_of(j * sub, sub), sub), :], xg[op], 1, 0)

            @pl.when(lax.rem(i, 2) == 0)
            def _():
                core_copy(op, yy).start()

            @pl.when(i == 1)
            def _():
                core_copy(op, 1 - y).wait_recv()
                sb[op] = part[op, j] + rsa[op, 1 - y]
                y_copy(op).start()

            return carry

        lax.fori_loop(0, col, step, 0)

    def product_end(op):
        core_copy(op, y).wait_recv()
        own = part[op, c] + rsa[op, y]
        y_copy(op).wait_recv()
        yv[op] = own + rsb[op]
        core_copy(op, 0).wait_send()
        core_copy(op, 1).wait_send()
        y_copy(op).wait_send()

    def c1(op):
        return rcopy(gp.at[op, pl.ds((1 - k) * half, half)], g1.at[op], g1_ss.at[op], g1_rs.at[op], partner)

    def c2(op):
        return rcopy(s1.at[op, pl.ds((1 - y) * quarter, quarter)], g2.at[op], g2_ss.at[op], g2_rs.at[op], across)

    chip, chips = 2 * z + y, 2 * rows

    def c3(op, turn, d, mine):
        other = lax.rem(chip + d, chips)
        at = chip if mine else other
        place = slots.at[op, turn, at]
        return rcopy(place, place, sl_ss.at[op, d], sl_rs.at[op, turn, at], dev(other // 2, lax.rem(other, 2), k))

    def c4(op):
        rng = pl.ds(k * half, half)
        return rcopy(gs.at[op, rng], gs.at[op, rng], g4_ss.at[op], g4_rs.at[op], partner)

    def c4_in(op):
        rng = pl.ds((1 - k) * half, half)
        return rcopy(gs.at[op, rng], gs.at[op, rng], g4_ss.at[op], g4_rs.at[op], partner)

    def sum_rest(ops, turn):
        for op in ops:
            c1(op).wait_recv()
            s1[op] = gp[op, pl.ds(pl.multiple_of(k * half, half), half), :] + g1[op]
            c2(op).start()
        for op in ops:
            c2(op).wait_recv()
            slots[op, turn, chip] = s1[op, pl.ds(pl.multiple_of(y * quarter, quarter), quarter), :] + g2[op]
            for d in range(1, chips):
                c3(op, turn, d, True).start()
        for op in ops:
            for d in range(1, chips):
                c3(op, turn, d, False).wait_recv()
            for yy in range(2):
                acc = slots[op, turn, yy]
                for zz in range(1, rows):
                    acc = acc + slots[op, turn, 2 * zz + yy]
                gs[op, pl.ds(pl.multiple_of(k * half + yy * quarter, quarter), quarter), :] = acc
            c4(op).start()
        for op in ops:
            c4_in(op).wait_recv()
            c1(op).wait_send()
            c2(op).wait_send()
            for d in range(1, chips):
                c3(op, turn, d, True).wait_send()
            c4(op).wait_send()

    lane = lax.broadcasted_iota(jnp.int32, (8, 128), 1)
    sublane = lax.broadcasted_iota(jnp.int32, (8, 128), 0)

    def factor(ops):
        eye = (lax.broadcasted_iota(jnp.int32, (128, 128), 0) == lax.broadcasted_iota(jnp.int32, (128, 128), 1)).astype(F32)
        for op in ops:
            gw[op, :, 0:128] = gs[op] / total
            gw[op, :, 128:256] = eye

        def step(i, carry):
            rng = pl.ds(pl.multiple_of(i * 8, 8), 8)
            for op in ops:
                p0, p1 = gw[op, rng, 0:128], gw[op, rng, 128:256]
                cols = []
                for j in range(8):
                    one = jnp.sum(jnp.where(lane == i * 8 + j, p0, 0.0), axis=1, keepdims=True)
                    cols.append(jnp.broadcast_to(one, (8, 128)))
                pivots = jnp.ones((8, 128), F32)
                for j in range(8):
                    d = jnp.broadcast_to(cols[j][j:j + 1], (8, 128))
                    pivots = jnp.where(sublane == j, d, pivots)
                    if j < 7:
                        m = jnp.where(sublane > j, cols[j] * (1.0 / d), 0.0)
                        p0 = p0 - m * jnp.broadcast_to(p0[j:j + 1], (8, 128))
                        p1 = p1 - m * jnp.broadcast_to(p1[j:j + 1], (8, 128))
                        for q in range(j + 1, 8):
                            cols[q] = cols[q] - m * jnp.broadcast_to(cols[q][j:j + 1], (8, 128))
                scale = lax.rsqrt(pivots)
                p0, p1 = p0 * scale, p1 * scale
                mv[op, rng, :] = p1
                l1, l2, l3 = split3(p0)
                r1, r2, r3 = split3(jnp.concatenate([p0, p1], axis=1))
                lhs = jnp.concatenate([l1, l1, l2, l1, l2, l3], axis=0).astype(BF16)
                rhs = jnp.concatenate([r1, r2, r1, r3, r2, r1], axis=0).astype(BF16)
                gw[op] = gw[op] - dot(lhs, rhs, 0, 0)
            return carry

        lax.fori_loop(0, 16, step, 0)

    for op in OPS:
        xz[op, z] = (left_start, right_start)[op][...].astype(BF16)
        spread_begin(op)
    for t in range(1, rows):
        for op in OPS:
            spread_step(op, t)
    for op in OPS:
        for j in range(col):
            load(op, j).wait()

    def products():
        for op in OPS:
            spread_end(op)
            product(op)
            spread_sent(op)

    def sweep(s, carry):
        products()
        for op in OPS:
            product_end(op)
            y_half = yv[op].astype(BF16)
            gp[op] = dot(y_half, y_half, 0, 0)
            c1(op).start()
        sum_rest(OPS, 0)
        factor(OPS)
        for op in OPS:
            y_one = dot(yv[op], mv[op], 1, 1, HIGHEST)
            yv[op] = y_one
            gp[op] = dot(y_one, y_one, 0, 0, HIGHEST)
            c1(op).start()
        sum_rest(OPS, 1)
        factor(OPS)
        for op in OPS:
            x = dot(yv[op], mv[op], 1, 1, HIGHEST)
            xf[op] = x
            xz[op, z] = x.astype(BF16)
            spread_begin(op)
        for t in range(1, rows):
            for op in OPS:
                spread_step(op, t)
        return carry

    lax.fori_loop(0, SWEEPS, sweep, 0)
    left_basis[...] = xf[0]
    right_basis[...] = xf[1]
    products()
    for op in OPS:
        product_end(op)
        gp[op] = dot(xf[op], yv[op], 0, 0, HIGHEST)
        c1(op).start()
    sum_rest(OPS, 0)
    left_ray[...] = gs[0] / total
    right_ray[...] = gs[1] / total


def solution(mesh):
    rows, col = mesh.shape["row"], mesh.shape["col"]

    def local_program(left_op, left_start, right_op, right_start):
        blk, s = left_op.shape[0], left_start.shape[1]
        sub = left_start.shape[0]
        vmem = pl.BlockSpec(memory_space=pltpu.VMEM)
        hbm = pl.BlockSpec(memory_space=pl.ANY)
        basis = jax.ShapeDtypeStruct((sub, s), F32)
        ray = jax.ShapeDtypeStruct((s, s), F32)
        dma = pltpu.SemaphoreType.DMA
        scratch = [
            pltpu.VMEM((2, blk, blk), BF16),
            pltpu.VMEM((2, blk, s), BF16),
            pltpu.VMEM((2, rows, sub, s), BF16),
            pltpu.VMEM((2, sub, s), F32),
            pltpu.VMEM((2, col, sub, s), F32),
            pltpu.VMEM((2, 2, sub, s), F32),
            pltpu.VMEM((2, sub, s), F32),
            pltpu.VMEM((2, sub, s), F32),
            pltpu.VMEM((2, sub, s), F32),
            pltpu.VMEM((2, s, s), F32),
            pltpu.VMEM((2, s // 2, s), F32),
            pltpu.VMEM((2, s // 2, s), F32),
            pltpu.VMEM((2, s // 4, s), F32),
            pltpu.VMEM((2, 2, 2 * rows, s // 4, s), F32),
            pltpu.VMEM((2, s, s), F32),
            pltpu.VMEM((2, s, 2 * s), F32),
            pltpu.VMEM((2, s, s), F32),
            dma((2, col)),
            dma((2, 2)), dma((2, 2)), dma((2,)), dma((2,)),
            dma((2,)), dma((2,)), dma((2,)), dma((2,)),
            dma((2, 2 * rows)), dma((2, 2, 2 * rows)), dma((2,)), dma((2,)),
            dma((2, rows, CHUNKS)), dma((2, rows, CHUNKS)), dma((2, rows, CHUNKS)),
            dma((2, rows, CHUNKS)), dma((2, col, CHUNKS)),
        ]
        return pl.pallas_call(
            functools.partial(kernel, rows, col),
            out_shape=(basis, ray, basis, ray),
            in_specs=[hbm, vmem, hbm, vmem],
            out_specs=(vmem,) * 4,
            scratch_shapes=scratch,
            compiler_params=pltpu.CompilerParams(collective_id=0, has_side_effects=True, vmem_limit_bytes=66_000_000),
        )(left_op, left_start, right_op, right_start)

    op_spec = P(("batch", "row"), "col")
    vec_spec = P(("batch", "row", "col"), None)
    small_spec = P("batch", None)
    return jax.shard_map(local_program, mesh=mesh, in_specs=(op_spec, vec_spec, op_spec, vec_spec), out_specs=(vec_spec, small_spec, vec_spec, small_spec), check_vma=False)
```

time: 1840 us -> 473 us (0.26)
  waiting for transfers between devices: 956 us -> 0 us
  Pallas kernels: 0 us -> 466 us
  other arithmetic: 389 us -> 0 us
  blocking collectives: 286 us -> 0 us
  matrix products: 176 us -> 0 us
    psum x9 -> x0, waiting for transfers between devices: 822 us -> none  [gram_total(): return lax.psum(local_gram, grid_axes)]
    pallas_call x0 -> x1, Pallas kernels: none -> 466 us  [local_program(): pl.pallas_call(functools.partial(kernel, rows, col), out_shape=(basis, ra...]
    another operation x80 -> x0, other arithmetic: 367 us -> none  [the longest x48 198 us: cholqr_step(): chol_low = jnp.linalg.cholesky(gram_mat)]
    all_gather x10 -> x0, blocking collectives: 286 us -> none  [apply_op(): x_col = lax.all_gather(x_moved, 'row', axis=0, tiled=True)]
    dot_general x28 -> x0, matrix products: 160 us -> none  [the longest x10 131 us: apply_op(): partial_prod = jnp.dot(op_blk, x_col, preferred_element_type=jnp.float32)]
    reduce_scatter x10 -> x0, waiting for transfers between devices: 133 us -> none  [apply_op(): lax.psum_scatter(partial_prod, 'col', scatter_dimension=0, tiled=True)]
    div x33 -> x0, other arithmetic: 21.5 us -> none  [the longest x15 9.53 us: cholqr_step(): chol_low = jnp.linalg.cholesky(gram_mat)]
  transfers between devices with their start and end apart: 29 -> 0, of which waited for: 14 -> 0; matrix products, arithmetic and copies ran while one was open for 9% -> 0% of each run, Pallas kernels for 0% -> 0%
where the time goes in v1:
time: 473 us
  Pallas kernels  466 us (99%)
  local copies, waits for them, and re-layouts  6.48 us (1%)
    pallas_call x1, Pallas kernels, local_program(): pl.pallas_call(functools.partial(kernel, rows, col), out_shape=(basis, ra...  466 us

profile of v1, /device:TPU:0, one launch (start us, length us, event | category | flops | bytes accessed | tf_op | source)
XLA Modules:
  0.0 472.8 jit_solution(6495150966200553755)
XLA Ops:
  0.6 465.7 %shard_map.75 = (f32[768,128]{1,0:T(8,128)}, f32[128,128]{1,0:T(8,128)}, f32[768,128]{1,0:T(8,128)}, f32[128,128]{1,0:T(8,128)}) custom-call(bf16[3072,3072]{1,0:T(8,128)(2,1)} %left_op.1, f32[768,128]{1,0:T(8,128)} %left_start.1, bf16[3072,3072]{1,0:T(8,128)(2,1)} %right_op.1, f32[768,128]{1,0:T(8,128)} %right_start.1), custom_call_target="tpu_custom_call" | custom-call | tf_op jit(solution)/shard_map/pallas_call | solution.py:364
  466.3 1.8 copy.12
  468.1 1.5 copy.13
  469.5 1.8 copy.14
  471.3 1.5 copy.15

commit v2 on v1

--- a/solution.py
+++ b/solution.py
@@ -9,6 +9,7 @@
 
 SWEEPS = 4
 CHUNKS = 2
+PARTS = 4
 MESH = pl.DeviceIdType.MESH
 HIGHEST = lax.Precision.HIGHEST
 OPS = (0, 1)
@@ -29,7 +30,7 @@
 
 
 def kernel(rows, col, left_op, left_start, right_op, right_start, left_basis, left_ray, right_basis, right_ray,
-           a_v, xg, xz, xf, part, rsa, sb, rsb, yv, gp, g1, s1, g2, slots, gs, gw, mv,
+           a_v, xg, xz, xf, part, rsa, sb, rsb, yv, gp, g1, s1, g2, slots, gs, gw, mv, keep,
            load_sem, rsa_ss, rsa_rs, rsb_ss, rsb_rs, g1_ss, g1_rs, g2_ss, g2_rs, sl_ss, sl_rs, g4_ss, g4_rs,
            zr_ss, zl_ss, z_rs, p_ss, p_rs):
     b, z, c = lax.axis_index("batch"), lax.axis_index("row"), lax.axis_index("col")
@@ -101,29 +102,28 @@
         for h in range(CHUNKS):
             p_start(op, z, h)
 
-    def spread_step(op, t):
-        for h in range(CHUNKS):
-            @pl.when(z - t >= 0)
+    def spread_step(op, t, h):
+        @pl.when(z - t >= 0)
+        def _():
+            slot = z - t
+            z_copy(op, slot, h, 1).wait_recv()
+
+            @pl.when(z < rows - 1)
             def _():
-                slot = z - t
-                z_copy(op, slot, h, 1).wait_recv()
-
-                @pl.when(z < rows - 1)
-                def _():
-                    z_copy(op, slot, h, 1).start()
-
-                p_start(op, slot, h)
-
-            @pl.when(z + t < rows)
+                z_copy(op, slot, h, 1).start()
+
+            p_start(op, slot, h)
+
+        @pl.when(z + t < rows)
+        def _():
+            slot = z + t
+            z_copy(op, slot, h, -1).wait_recv()
+
+            @pl.when(z > 0)
             def _():
-                slot = z + t
-                z_copy(op, slot, h, -1).wait_recv()
-
-                @pl.when(z > 0)
-                def _():
-                    z_copy(op, slot, h, -1).start()
-
-                p_start(op, slot, h)
+                z_copy(op, slot, h, -1).start()
+
+            p_start(op, slot, h)
 
     def spread_end(op):
         for src in range(col):
@@ -152,26 +152,16 @@
     def y_copy(op):
         return rcopy(sb.at[op], rsb.at[op], rsb_ss.at[op], rsb_rs.at[op], across)
 
-    def product(op):
-        def step(i, carry):
-            yy = (1 - y) + (i // 2) * (2 * y - 1)
-            kk = (1 - k) + lax.rem(i, 2) * (2 * k - 1)
-            j = 2 * yy + kk
-            part[op, j] = dot(a_v[op, pl.ds(pl.multiple_of(j * sub, sub), sub), :], xg[op], 1, 0)
-
-            @pl.when(lax.rem(i, 2) == 0)
-            def _():
-                core_copy(op, yy).start()
-
-            @pl.when(i == 1)
-            def _():
-                core_copy(op, 1 - y).wait_recv()
-                sb[op] = part[op, j] + rsa[op, 1 - y]
-                y_copy(op).start()
-
-            return carry
-
-        lax.fori_loop(0, col, step, 0)
+    def product(op, i):
+        yy, kk = (1 - y, y)[i // 2], (1 - k, k)[i % 2]
+        j = 2 * yy + kk
+        part[op, j] = dot(a_v[op, pl.ds(pl.multiple_of(j * sub, sub), sub), :], xg[op], 1, 0)
+        if i % 2 == 0:
+            core_copy(op, yy).start()
+        if i == 1:
+            core_copy(op, yy).wait_recv()
+            sb[op] = part[op, j] + rsa[op, yy]
+            y_copy(op).start()
 
     def product_end(op):
         core_copy(op, y).wait_recv()
@@ -204,125 +194,152 @@
         rng = pl.ds((1 - k) * half, half)
         return rcopy(gs.at[op, rng], gs.at[op, rng], g4_ss.at[op], g4_rs.at[op], partner)
 
-    def sum_rest(ops, turn):
-        for op in ops:
-            c1(op).wait_recv()
-            s1[op] = gp[op, pl.ds(pl.multiple_of(k * half, half), half), :] + g1[op]
-            c2(op).start()
-        for op in ops:
-            c2(op).wait_recv()
-            slots[op, turn, chip] = s1[op, pl.ds(pl.multiple_of(y * quarter, quarter), quarter), :] + g2[op]
-            for d in range(1, chips):
-                c3(op, turn, d, True).start()
-        for op in ops:
-            for d in range(1, chips):
-                c3(op, turn, d, False).wait_recv()
-            for yy in range(2):
-                acc = slots[op, turn, yy]
-                for zz in range(1, rows):
-                    acc = acc + slots[op, turn, 2 * zz + yy]
-                gs[op, pl.ds(pl.multiple_of(k * half + yy * quarter, quarter), quarter), :] = acc
-            c4(op).start()
-        for op in ops:
-            c4_in(op).wait_recv()
-            c1(op).wait_send()
-            c2(op).wait_send()
-            for d in range(1, chips):
-                c3(op, turn, d, True).wait_send()
-            c4(op).wait_send()
+    def group_sum(op, turn):
+        c1(op).start()
+        yield
+        c1(op).wait_recv()
+        s1[op] = gp[op, pl.ds(pl.multiple_of(k * half, half), half), :] + g1[op]
+        c2(op).start()
+        yield
+        c2(op).wait_recv()
+        slots[op, turn, chip] = s1[op, pl.ds(pl.multiple_of(y * quarter, quarter), quarter), :] + g2[op]
+        for d in range(1, chips):
+            c3(op, turn, d, True).start()
+        yield
+        for d in range(1, chips):
+            c3(op, turn, d, False).wait_recv()
+        for yy in range(2):
+            acc = slots[op, turn, yy]
+            for zz in range(1, rows):
+                acc = acc + slots[op, turn, 2 * zz + yy]
+            gs[op, pl.ds(pl.multiple_of(k * half + yy * quarter, quarter), quarter), :] = acc
+        c4(op).start()
+        yield
+        c4_in(op).wait_recv()
+        c1(op).wait_send()
+        c2(op).wait_send()
+        for d in range(1, chips):
+            c3(op, turn, d, True).wait_send()
+        c4(op).wait_send()
 
     lane = lax.broadcasted_iota(jnp.int32, (8, 128), 1)
     sublane = lax.broadcasted_iota(jnp.int32, (8, 128), 0)
 
-    def factor(ops):
+    def spread_row(v, j):
+        return jnp.broadcast_to(v[j:j + 1], (8, 128))
+
+    def panel(op, i, state):
+        p0, p1, q0, q1 = state
+        now = pl.ds(pl.multiple_of(i * 8, 8), 8)
+        following = jnp.minimum(i + 1, 15) * 8
+        cols = []
+        for base in (i * 8, following):
+            for j in range(8):
+                one = jnp.sum(jnp.where(lane == base + j, p0, 0.0), axis=1, keepdims=True)
+                cols.append(jnp.broadcast_to(one, (8, 128)))
+        l1, l2, l3 = split3(q0)
+        r1, r2, r3 = split3(jnp.concatenate([q0, q1], axis=1))
+        lhs = jnp.concatenate([l1, l1, l2, l1, l2, l3], axis=0).astype(BF16)
+        rhs = jnp.concatenate([r1, r2, r1, r3, r2, r1], axis=0).astype(BF16)
+        gw[op] = gw[op] - dot(lhs, rhs, 0, 0)
+        scale = jnp.ones((8, 128), F32)
+        for j in range(8):
+            root = lax.rsqrt(spread_row(cols[j], j))
+            scale = jnp.where(sublane == j, root, scale)
+            if j < 7:
+                m = jnp.where(sublane > j, cols[j] * (root * root), 0.0)
+                for q in range(j + 1, 16):
+                    cols[q] = cols[q] - m * spread_row(cols[q], j)
+                p0 = p0 - m * spread_row(p0, j)
+                p1 = p1 - m * spread_row(p1, j)
+        p0, p1 = p0 * scale, p1 * scale
+        mv[op, now, :] = p1
+        s0, s1_ = jnp.zeros((8, 128), F32), jnp.zeros((8, 128), F32)
+        for j in range(8):
+            w = cols[8 + j] * scale
+            s0 = jnp.where(sublane == j, jnp.sum(w * p0, axis=0, keepdims=True), s0)
+            s1_ = jnp.where(sublane == j, jnp.sum(w * p1, axis=0, keepdims=True), s1_)
+        rng = pl.ds(pl.multiple_of(following, 8), 8)
+        return gw[op, rng, 0:128] - s0, gw[op, rng, 128:256] - s1_, p0, p1
+
+    def factor(op):
         eye = (lax.broadcasted_iota(jnp.int32, (128, 128), 0) == lax.broadcasted_iota(jnp.int32, (128, 128), 1)).astype(F32)
-        for op in ops:
-            gw[op, :, 0:128] = gs[op] / total
-            gw[op, :, 128:256] = eye
-
-        def step(i, carry):
-            rng = pl.ds(pl.multiple_of(i * 8, 8), 8)
-            for op in ops:
-                p0, p1 = gw[op, rng, 0:128], gw[op, rng, 128:256]
-                cols = []
-                for j in range(8):
-                    one = jnp.sum(jnp.where(lane == i * 8 + j, p0, 0.0), axis=1, keepdims=True)
-                    cols.append(jnp.broadcast_to(one, (8, 128)))
-                pivots = jnp.ones((8, 128), F32)
-                for j in range(8):
-                    d = jnp.broadcast_to(cols[j][j:j + 1], (8, 128))
-                    pivots = jnp.where(sublane == j, d, pivots)
-                    if j < 7:
-                        m = jnp.where(sublane > j, cols[j] * (1.0 / d), 0.0)
-                        p0 = p0 - m * jnp.broadcast_to(p0[j:j + 1], (8, 128))
-                        p1 = p1 - m * jnp.broadcast_to(p1[j:j + 1], (8, 128))
-                        for q in range(j + 1, 8):
-                            cols[q] = cols[q] - m * jnp.broadcast_to(cols[q][j:j + 1], (8, 128))
-                scale = lax.rsqrt(pivots)
-                p0, p1 = p0 * scale, p1 * scale
-                mv[op, rng, :] = p1
-                l1, l2, l3 = split3(p0)
-                r1, r2, r3 = split3(jnp.concatenate([p0, p1], axis=1))
-                lhs = jnp.concatenate([l1, l1, l2, l1, l2, l3], axis=0).astype(BF16)
-                rhs = jnp.concatenate([r1, r2, r1, r3, r2, r1], axis=0).astype(BF16)
-                gw[op] = gw[op] - dot(lhs, rhs, 0, 0)
-            return carry
-
-        lax.fori_loop(0, 16, step, 0)
-
-    for op in OPS:
-        xz[op, z] = (left_start, right_start)[op][...].astype(BF16)
+        g = gs[op] / total
+        gw[op, :, 0:128] = g
+        gw[op, :, 128:256] = eye
+        zero = jnp.zeros((8, 128), F32)
+        state = (g[0:8], eye[0:8], zero, zero)
+        for part_no in range(PARTS):
+            if part_no:
+                yield
+                state = tuple(keep[op, i] for i in range(4))
+            n = 16 // PARTS
+            state = lax.fori_loop(n * part_no, n * part_no + n, lambda i, st: panel(op, i, st), state)
+            if part_no < PARTS - 1:
+                for i in range(4):
+                    keep[op, i] = state[i]
+
+    def transport(op, first=False):
         spread_begin(op)
-    for t in range(1, rows):
-        for op in OPS:
-            spread_step(op, t)
-    for op in OPS:
-        for j in range(col):
-            load(op, j).wait()
-
-    def products():
-        for op in OPS:
-            spread_end(op)
-            product(op)
-            spread_sent(op)
+        yield
+        for t in range(1, rows):
+            for h in range(CHUNKS):
+                spread_step(op, t, h)
+                yield
+        if first:
+            for j in range(col):
+                load(op, j).wait()
+        spread_end(op)
+        for i in range(4):
+            product(op, i)
+            yield
+        spread_sent(op)
+        product_end(op)
+
+    def ortho(op):
+        y_half = yv[op].astype(BF16)
+        gp[op] = dot(y_half, y_half, 0, 0)
+        yield from group_sum(op, 0)
+        yield from factor(op)
+        yield
+        y_one = dot(yv[op], mv[op], 1, 1, HIGHEST)
+        yv[op] = y_one
+        gp[op] = dot(y_one, y_one, 0, 0, HIGHEST)
+        yield from group_sum(op, 1)
+        yield from factor(op)
+        x = dot(yv[op], mv[op], 1, 1, HIGHEST)
+        xf[op] = x
+        xz[op, z] = x.astype(BF16)
+
+    def rayleigh(op):
+        gp[op] = dot(xf[op], yv[op], 0, 0, HIGHEST)
+        yield from group_sum(op, 0)
+        (left_ray, right_ray)[op][...] = gs[op] / total
+
+    def run(order, **streams):
+        for name in order:
+            next(streams[name], None)
+        for stream in streams.values():
+            for _ in stream:
+                pass
+
+    ORDER = "TOOOTTTTOOTOOTOOTOTTOTOOOOO"
+    xz[0, z] = left_start[...].astype(BF16)
+    xz[1, z] = right_start[...].astype(BF16)
+    run("", T=transport(0, True))
+    for j in range(col):
+        load(1, j).wait()
 
     def sweep(s, carry):
-        products()
-        for op in OPS:
-            product_end(op)
-            y_half = yv[op].astype(BF16)
-            gp[op] = dot(y_half, y_half, 0, 0)
-            c1(op).start()
-        sum_rest(OPS, 0)
-        factor(OPS)
-        for op in OPS:
-            y_one = dot(yv[op], mv[op], 1, 1, HIGHEST)
-            yv[op] = y_one
-            gp[op] = dot(y_one, y_one, 0, 0, HIGHEST)
-            c1(op).start()
-        sum_rest(OPS, 1)
-        factor(OPS)
-        for op in OPS:
-            x = dot(yv[op], mv[op], 1, 1, HIGHEST)
-            xf[op] = x
-            xz[op, z] = x.astype(BF16)
-            spread_begin(op)
-        for t in range(1, rows):
-            for op in OPS:
-                spread_step(op, t)
+        run(ORDER, O=ortho(0), T=transport(1))
+        run(ORDER, O=ortho(1), T=transport(0))
         return carry
 
     lax.fori_loop(0, SWEEPS, sweep, 0)
     left_basis[...] = xf[0]
     right_basis[...] = xf[1]
-    products()
-    for op in OPS:
-        product_end(op)
-        gp[op] = dot(xf[op], yv[op], 0, 0, HIGHEST)
-        c1(op).start()
-    sum_rest(OPS, 0)
-    left_ray[...] = gs[0] / total
-    right_ray[...] = gs[1] / total
+    run("TOOOTTTTOO", O=rayleigh(0), T=transport(1))
+    run("", O=rayleigh(1))
 
 
 def solution(mesh):
@@ -354,6 +371,7 @@
             pltpu.VMEM((2, s, s), F32),
             pltpu.VMEM((2, s, 2 * s), F32),
             pltpu.VMEM((2, s, s), F32),
+            pltpu.VMEM((2, 4, 8, s), F32),
             dma((2, col)),
             dma((2, 2)), dma((2, 2)), dma((2,)), dma((2,)),
             dma((2,)), dma((2,)), dma((2,)), dma((2,)),

time: 473 us -> 428 us (0.905)
  Pallas kernels: 466 us -> 421 us
    pallas_call x1, Pallas kernels: 466 us -> 421 us  [local_program(): pl.pallas_call(functools.partial(kernel, rows, col), out_shape=(basis, ra...]
where the time goes in v2:
time: 428 us
  Pallas kernels  421 us (98%)
  local copies, waits for them, and re-layouts  6.48 us (2%)
    pallas_call x1, Pallas kernels, local_program(): pl.pallas_call(functools.partial(kernel, rows, col), out_shape=(basis, ra...  421 us

profile of v2, /device:TPU:0, one launch (start us, length us, event | category | flops | bytes accessed | tf_op | source)
XLA Modules:
  0.0 427.8 jit_solution(745387979727843533)
XLA Ops:
  0.6 420.6 %shard_map.75 = (f32[768,128]{1,0:T(8,128)}, f32[128,128]{1,0:T(8,128)}, f32[768,128]{1,0:T(8,128)}, f32[128,128]{1,0:T(8,128)}) custom-call(bf16[3072,3072]{1,0:T(8,128)(2,1)} %left_op.1, f32[768,128]{1,0:T(8,128)} %left_start.1, bf16[3072,3072]{1,0:T(8,128)(2,1)} %right_op.1, f32[768,128]{1,0:T(8,128)} %right_start.1), custom_call_target="tpu_custom_call" | custom-call | tf_op jit(solution)/shard_map/pallas_call | solution.py:382
  421.3 1.8 copy.12
  423.0 1.5 copy.13
  424.5 1.8 copy.14
  426.3 1.5 copy.15

commit v3 on v2

--- a/solution.py
+++ b/solution.py
@@ -39,7 +39,6 @@
     sub = blk // col
     piece = sub // CHUNKS
     total = blk * rows
-    half, quarter = 64, 32
 
     def dev(zz, yy, kk):
         return (b, zz, 2 * yy + kk)
@@ -172,55 +171,54 @@
         core_copy(op, 1).wait_send()
         y_copy(op).wait_send()
 
-    def c1(op):
-        return rcopy(gp.at[op, pl.ds((1 - k) * half, half)], g1.at[op], g1_ss.at[op], g1_rs.at[op], partner)
-
-    def c2(op):
-        return rcopy(s1.at[op, pl.ds((1 - y) * quarter, quarter)], g2.at[op], g2_ss.at[op], g2_rs.at[op], across)
-
-    chip, chips = 2 * z + y, 2 * rows
-
-    def c3(op, turn, d, mine):
-        other = lax.rem(chip + d, chips)
-        at = chip if mine else other
-        place = slots.at[op, turn, at]
-        return rcopy(place, place, sl_ss.at[op, d], sl_rs.at[op, turn, at], dev(other // 2, lax.rem(other, 2), k))
-
-    def c4(op):
-        rng = pl.ds(k * half, half)
-        return rcopy(gs.at[op, rng], gs.at[op, rng], g4_ss.at[op], g4_rs.at[op], partner)
-
-    def c4_in(op):
-        rng = pl.ds((1 - k) * half, half)
-        return rcopy(gs.at[op, rng], gs.at[op, rng], g4_ss.at[op], g4_rs.at[op], partner)
-
-    def group_sum(op, turn):
-        c1(op).start()
-        yield
-        c1(op).wait_recv()
-        s1[op] = gp[op, pl.ds(pl.multiple_of(k * half, half), half), :] + g1[op]
-        c2(op).start()
-        yield
-        c2(op).wait_recv()
-        slots[op, turn, chip] = s1[op, pl.ds(pl.multiple_of(y * quarter, quarter), quarter), :] + g2[op]
-        for d in range(1, chips):
-            c3(op, turn, d, True).start()
-        yield
-        for d in range(1, chips):
-            c3(op, turn, d, False).wait_recv()
-        for yy in range(2):
-            acc = slots[op, turn, yy]
-            for zz in range(1, rows):
-                acc = acc + slots[op, turn, 2 * zz + yy]
-            gs[op, pl.ds(pl.multiple_of(k * half + yy * quarter, quarter), quarter), :] = acc
-        c4(op).start()
-        yield
-        c4_in(op).wait_recv()
-        c1(op).wait_send()
-        c2(op).wait_send()
-        for d in range(1, chips):
-            c3(op, turn, d, True).wait_send()
-        c4(op).wait_send()
+    def group_sum(op, turn, size):
+        half, quarter = size // 2, size // 4
+
+        def rng(which, length):
+            return pl.ds(pl.multiple_of(which * length, length), length)
+
+        c1 = rcopy(gp.at[op, rng(1 - k, half)], g1.at[op, pl.ds(0, half)], g1_ss.at[op], g1_rs.at[op], partner)
+        c2 = rcopy(s1.at[op, rng(1 - y, quarter)], g2.at[op, pl.ds(0, quarter)], g2_ss.at[op], g2_rs.at[op], across)
+        c4 = rcopy(gs.at[op, rng(k, half)], gs.at[op, rng(k, half)], g4_ss.at[op], g4_rs.at[op], partner)
+        c4_in = rcopy(gs.at[op, rng(1 - k, half)], gs.at[op, rng(1 - k, half)], g4_ss.at[op], g4_rs.at[op], partner)
+        chip, chips = 2 * z + y, 2 * rows
+
+        def c3(d, mine):
+            other = lax.rem(chip + d, chips)
+            at = chip if mine else other
+            place = slots.at[op, turn, at, pl.ds(0, quarter)]
+            return rcopy(place, place, sl_ss.at[op, d], sl_rs.at[op, turn, at], dev(other // 2, lax.rem(other, 2), k))
+
+        def over_cores():
+            c1.wait_recv()
+            s1[op, 0:half] = gp[op, rng(k, half), :] + g1[op, 0:half]
+            c2.start()
+
+        def over_y():
+            c2.wait_recv()
+            slots[op, turn, chip, 0:quarter] = s1[op, rng(y, quarter), :] + g2[op, 0:quarter]
+            for d in range(1, chips):
+                c3(d, True).start()
+
+        def over_chips():
+            for d in range(1, chips):
+                c3(d, False).wait_recv()
+            for yy in range(2):
+                acc = slots[op, turn, yy, 0:quarter]
+                for zz in range(1, rows):
+                    acc = acc + slots[op, turn, 2 * zz + yy, 0:quarter]
+                gs[op, pl.ds(pl.multiple_of(k * half + yy * quarter, quarter), quarter), :] = acc
+            c4.start()
+
+        def finish():
+            c4_in.wait_recv()
+            c1.wait_send()
+            c2.wait_send()
+            for d in range(1, chips):
+                c3(d, True).wait_send()
+            c4.wait_send()
+
+        return c1.start, over_cores, over_y, over_chips, finish
 
     lane = lax.broadcasted_iota(jnp.int32, (8, 128), 1)
     sublane = lax.broadcasted_iota(jnp.int32, (8, 128), 0)
@@ -263,12 +261,8 @@
         return gw[op, rng, 0:128] - s0, gw[op, rng, 128:256] - s1_, p0, p1
 
     def factor(op):
-        eye = (lax.broadcasted_iota(jnp.int32, (128, 128), 0) == lax.broadcasted_iota(jnp.int32, (128, 128), 1)).astype(F32)
-        g = gs[op] / total
-        gw[op, :, 0:128] = g
-        gw[op, :, 128:256] = eye
         zero = jnp.zeros((8, 128), F32)
-        state = (g[0:8], eye[0:8], zero, zero)
+        state = (gw[op, 0:8, 0:128], gw[op, 0:8, 128:256], zero, zero)
         for part_no in range(PARTS):
             if part_no:
                 yield
@@ -279,13 +273,13 @@
                 for i in range(4):
                     keep[op, i] = state[i]
 
-    def transport(op, first=False):
-        spread_begin(op)
-        yield
-        for t in range(1, rows):
-            for h in range(CHUNKS):
-                spread_step(op, t, h)
-                yield
+    def eye():
+        return (lax.broadcasted_iota(jnp.int32, (128, 128), 0) == lax.broadcasted_iota(jnp.int32, (128, 128), 1)).astype(F32)
+
+    def transport(op, done, first=False):
+        for n in range(done, (rows - 1) * CHUNKS):
+            spread_step(op, n // CHUNKS + 1, n % CHUNKS)
+            yield
         if first:
             for j in range(col):
                 load(op, j).wait()
@@ -296,50 +290,103 @@
         spread_sent(op)
         product_end(op)
 
-    def ortho(op):
-        y_half = yv[op].astype(BF16)
-        gp[op] = dot(y_half, y_half, 0, 0)
-        yield from group_sum(op, 0)
+    def ortho(op, last):
+        y_cur = yv[op]
+        y_half = y_cur.astype(BF16)
+        gp[op, 0:128] = dot(y_half, y_half, 0, 0)
+        gp[op, 128:256] = dot(y_cur, y_cur, 0, 0, HIGHEST)
+        steps = group_sum(op, 0, 256)
+        steps[0]()
+        for step in steps[1:-1]:
+            yield
+            step()
+        yield
+        steps[-1]()
+        gw[op, :, 0:128] = gs[op, 0:128] / total
+        gw[op, :, 128:256] = eye()
         yield from factor(op)
         yield
-        y_one = dot(yv[op], mv[op], 1, 1, HIGHEST)
-        yv[op] = y_one
-        gp[op] = dot(y_one, y_one, 0, 0, HIGHEST)
-        yield from group_sum(op, 1)
+        steps = group_sum(op, 1, 128)
+
+        @pl.when(last)
+        def _():
+            y_one = dot(yv[op], mv[op], 1, 1, HIGHEST)
+            yv[op] = y_one
+            gp[op, 0:128] = dot(y_one, y_one, 0, 0, HIGHEST)
+            steps[0]()
+
+        @pl.when(jnp.logical_not(last))
+        def _():
+            inv = mv[op]
+            gw[op, :, 0:128] = dot(dot(inv, gs[op, 128:256] / total, 1, 0, HIGHEST), inv, 1, 1, HIGHEST)
+            gw[op, :, 128:256] = inv
+
+        for step in steps[1:-1]:
+            yield
+            pl.when(last)(step)
+        yield
+
+        @pl.when(last)
+        def _():
+            steps[-1]()
+            gw[op, :, 0:128] = gs[op, 0:128] / total
+            gw[op, :, 128:256] = eye()
+
         yield from factor(op)
         x = dot(yv[op], mv[op], 1, 1, HIGHEST)
         xf[op] = x
         xz[op, z] = x.astype(BF16)
+        spread_begin(op)
 
     def rayleigh(op):
-        gp[op] = dot(xf[op], yv[op], 0, 0, HIGHEST)
-        yield from group_sum(op, 0)
-        (left_ray, right_ray)[op][...] = gs[op] / total
+        gp[op, 0:128] = dot(xf[op], yv[op], 0, 0, HIGHEST)
+        steps = group_sum(op, 0, 128)
+        steps[0]()
+        for step in steps[1:]:
+            yield
+            step()
+        (left_ray, right_ray)[op][...] = gs[op, 0:128] / total
 
     def run(order, **streams):
         for name in order:
             next(streams[name], None)
-        for stream in streams.values():
-            for _ in stream:
-                pass
-
-    ORDER = "TOOOTTTTOOTOOTOOTOTTOTOOOOO"
+
+    def rest(stream):
+        for _ in stream:
+            pass
+
+    def half_sweep(o_op, t_op, last):
+        o, t = ortho(o_op, last), transport(t_op, 1)
+        run("OTOTOTTTOTTOTTOOOOOOO", O=o, T=t)
+        rest(o)
+        spread_step(o_op, 1, 0)
+        rest(t)
+
     xz[0, z] = left_start[...].astype(BF16)
+    spread_begin(0)
     xz[1, z] = right_start[...].astype(BF16)
-    run("", T=transport(0, True))
+    t = transport(0, 0, True)
+    run("T" * ((rows - 1) * CHUNKS), T=t)
+    spread_begin(1)
+    run("TTTT", T=t)
+    spread_step(1, 1, 0)
+    rest(t)
     for j in range(col):
         load(1, j).wait()
 
     def sweep(s, carry):
-        run(ORDER, O=ortho(0), T=transport(1))
-        run(ORDER, O=ortho(1), T=transport(0))
+        half_sweep(0, 1, s == SWEEPS - 1)
+        half_sweep(1, 0, s == SWEEPS - 1)
         return carry
 
     lax.fori_loop(0, SWEEPS, sweep, 0)
     left_basis[...] = xf[0]
     right_basis[...] = xf[1]
-    run("TOOOTTTTOO", O=rayleigh(0), T=transport(1))
-    run("", O=rayleigh(1))
+    o, t = rayleigh(0), transport(1, 1)
+    run("OTOTOTTTOO", O=o, T=t)
+    rest(t)
+    rest(o)
+    rest(rayleigh(1))
 
 
 def solution(mesh):
@@ -363,12 +410,12 @@
             pltpu.VMEM((2, sub, s), F32),
             pltpu.VMEM((2, sub, s), F32),
             pltpu.VMEM((2, sub, s), F32),
+            pltpu.VMEM((2, 2 * s, s), F32),
+            pltpu.VMEM((2, s, s), F32),
             pltpu.VMEM((2, s, s), F32),
             pltpu.VMEM((2, s // 2, s), F32),
-            pltpu.VMEM((2, s // 2, s), F32),
-            pltpu.VMEM((2, s // 4, s), F32),
-            pltpu.VMEM((2, 2, 2 * rows, s // 4, s), F32),
-            pltpu.VMEM((2, s, s), F32),
+            pltpu.VMEM((2, 2, 2 * rows, s // 2, s), F32),
+            pltpu.VMEM((2, 2 * s, s), F32),
             pltpu.VMEM((2, s, 2 * s), F32),
             pltpu.VMEM((2, s, s), F32),
             pltpu.VMEM((2, 4, 8, s), F32),

time: 428 us -> 422 us (0.986)
  Pallas kernels: 421 us -> 415 us
    pallas_call x1, Pallas kernels: 421 us -> 415 us  [local_program(): pl.pallas_call(functools.partial(kernel, rows, col), out_shape=(basis, ra...]
where the time goes in v3:
time: 422 us
  Pallas kernels  415 us (98%)
  local copies, waits for them, and re-layouts  6.48 us (2%)
    pallas_call x1, Pallas kernels, local_program(): pl.pallas_call(functools.partial(kernel, rows, col), out_shape=(basis, ra...  415 us

profile of v3, /device:TPU:0, one launch (start us, length us, event | category | flops | bytes accessed | tf_op | source)
XLA Modules:
  0.0 421.8 jit_solution(5785141549307331325)
XLA Ops:
  0.6 414.7 %shard_map.75 = (f32[768,128]{1,0:T(8,128)}, f32[128,128]{1,0:T(8,128)}, f32[768,128]{1,0:T(8,128)}, f32[128,128]{1,0:T(8,128)}) custom-call(bf16[3072,3072]{1,0:T(8,128)(2,1)} %left_op.1, f32[768,128]{1,0:T(8,128)} %left_start.1, bf16[3072,3072]{1,0:T(8,128)(2,1)} %right_op.1, f32[768,128]{1,0:T(8,128)} %right_start.1), custom_call_target="tpu_custom_call" | custom-call | tf_op jit(solution)/shard_map/pallas_call | solution.py:429
  415.3 1.8 copy.12
  417.1 1.5 copy.13
  418.6 1.8 copy.14
  420.3 1.5 copy.15

commit v4 on v3

--- a/solution.py
+++ b/solution.py
@@ -276,8 +276,8 @@
     def eye():
         return (lax.broadcasted_iota(jnp.int32, (128, 128), 0) == lax.broadcasted_iota(jnp.int32, (128, 128), 1)).astype(F32)
 
-    def transport(op, done, first=False):
-        for n in range(done, (rows - 1) * CHUNKS):
+    def transport(op, first=False):
+        for n in range((rows - 1) * CHUNKS):
             spread_step(op, n // CHUNKS + 1, n % CHUNKS)
             yield
         if first:
@@ -288,9 +288,9 @@
             product(op, i)
             yield
         spread_sent(op)
+
+    def ortho(op, last):
         product_end(op)
-
-    def ortho(op, last):
         y_cur = yv[op]
         y_half = y_cur.astype(BF16)
         gp[op, 0:128] = dot(y_half, y_half, 0, 0)
@@ -339,6 +339,7 @@
         spread_begin(op)
 
     def rayleigh(op):
+        product_end(op)
         gp[op, 0:128] = dot(xf[op], yv[op], 0, 0, HIGHEST)
         steps = group_sum(op, 0, 128)
         steps[0]()
@@ -356,20 +357,17 @@
             pass
 
     def half_sweep(o_op, t_op, last):
-        o, t = ortho(o_op, last), transport(t_op, 1)
-        run("OTOTOTTTOTTOTTOOOOOOO", O=o, T=t)
+        o, t = ortho(o_op, last), transport(t_op)
+        run("OOTTOTTTOTOOTTOOOOTOTOOO", O=o, T=t)
+        rest(t)
         rest(o)
-        spread_step(o_op, 1, 0)
-        rest(t)
 
     xz[0, z] = left_start[...].astype(BF16)
     spread_begin(0)
     xz[1, z] = right_start[...].astype(BF16)
-    t = transport(0, 0, True)
+    t = transport(0, True)
     run("T" * ((rows - 1) * CHUNKS), T=t)
     spread_begin(1)
-    run("TTTT", T=t)
-    spread_step(1, 1, 0)
     rest(t)
     for j in range(col):
         load(1, j).wait()
@@ -382,8 +380,8 @@
     lax.fori_loop(0, SWEEPS, sweep, 0)
     left_basis[...] = xf[0]
     right_basis[...] = xf[1]
-    o, t = rayleigh(0), transport(1, 1)
-    run("OTOTOTTTOO", O=o, T=t)
+    o, t = rayleigh(0), transport(1)
+    run("OOTTOTTTOTO", O=o, T=t)
     rest(t)
     rest(o)
     rest(rayleigh(1))

time: 422 us -> 405 us (0.960)
  Pallas kernels: 415 us -> 398 us
    pallas_call x1, Pallas kernels: 415 us -> 398 us  [local_program(): pl.pallas_call(functools.partial(kernel, rows, col), out_shape=(basis, ra...]
where the time goes in v4:
time: 405 us
  Pallas kernels  398 us (98%)
  local copies, waits for them, and re-layouts  6.48 us (2%)
    pallas_call x1, Pallas kernels, local_program(): pl.pallas_call(functools.partial(kernel, rows, col), out_shape=(basis, ra...  398 us

profile of v4, /device:TPU:0, one launch (start us, length us, event | category | flops | bytes accessed | tf_op | source)
XLA Modules:
  0.0 405.0 jit_solution(10511415231526588659)
XLA Ops:
  0.6 397.8 %shard_map.75 = (f32[768,128]{1,0:T(8,128)}, f32[128,128]{1,0:T(8,128)}, f32[768,128]{1,0:T(8,128)}, f32[128,128]{1,0:T(8,128)}) custom-call(bf16[3072,3072]{1,0:T(8,128)(2,1)} %left_op.1, f32[768,128]{1,0:T(8,128)} %left_start.1, bf16[3072,3072]{1,0:T(8,128)(2,1)} %right_op.1, f32[768,128]{1,0:T(8,128)} %right_start.1), custom_call_target="tpu_custom_call" | custom-call | tf_op jit(solution)/shard_map/pallas_call | solution.py:427
  398.5 1.8 copy.12
  400.2 1.5 copy.13
  401.7 1.8 copy.14
  403.5 1.5 copy.15

commit v5 on v4

--- a/solution.py
+++ b/solution.py
@@ -154,7 +154,11 @@
     def product(op, i):
         yy, kk = (1 - y, y)[i // 2], (1 - k, k)[i % 2]
         j = 2 * yy + kk
-        part[op, j] = dot(a_v[op, pl.ds(pl.multiple_of(j * sub, sub), sub), :], xg[op], 1, 0)
+        upper, lower = (
+            dot(a_v[op, pl.ds(pl.multiple_of(j * sub + n * (sub // 2), sub // 2), sub // 2), :], xg[op], 1, 0) for n in range(2)
+        )
+        part[op, j, 0:sub // 2] = upper
+        part[op, j, sub // 2:sub] = lower
         if i % 2 == 0:
             core_copy(op, yy).start()
         if i == 1:

time: 405 us -> 374 us (0.923)
  Pallas kernels: 398 us -> 367 us
    pallas_call x1, Pallas kernels: 398 us -> 367 us  [local_program(): pl.pallas_call(functools.partial(kernel, rows, col), out_shape=(basis, ra...]
where the time goes in v5:
time: 374 us
  Pallas kernels  367 us (98%)
  local copies, waits for them, and re-layouts  6.48 us (2%)
    pallas_call x1, Pallas kernels, local_program(): pl.pallas_call(functools.partial(kernel, rows, col), out_shape=(basis, ra...  367 us

profile of v5, /device:TPU:0, one launch (start us, length us, event | category | flops | bytes accessed | tf_op | source)
XLA Modules:
  0.0 374.2 jit_solution(12200264872734847573)
XLA Ops:
  0.6 367.0 %shard_map.75 = (f32[768,128]{1,0:T(8,128)}, f32[128,128]{1,0:T(8,128)}, f32[768,128]{1,0:T(8,128)}, f32[128,128]{1,0:T(8,128)}) custom-call(bf16[3072,3072]{1,0:T(8,128)(2,1)} %left_op.1, f32[768,128]{1,0:T(8,128)} %left_start.1, bf16[3072,3072]{1,0:T(8,128)(2,1)} %right_op.1, f32[768,128]{1,0:T(8,128)} %right_start.1), custom_call_target="tpu_custom_call" | custom-call | tf_op jit(solution)/shard_map/pallas_call | solution.py:431
  367.7 1.8 copy.12
  369.4 1.5 copy.13
  370.9 1.8 copy.14
  372.7 1.5 copy.15

commit v6 on v5

--- a/solution.py
+++ b/solution.py
@@ -8,7 +8,7 @@
 from jax.sharding import PartitionSpec as P
 
 SWEEPS = 4
-CHUNKS = 2
+CHUNKS = 3
 PARTS = 4
 MESH = pl.DeviceIdType.MESH
 HIGHEST = lax.Precision.HIGHEST
@@ -337,9 +337,11 @@
             gw[op, :, 128:256] = eye()
 
         yield from factor(op)
-        x = dot(yv[op], mv[op], 1, 1, HIGHEST)
-        xf[op] = x
-        xz[op, z] = x.astype(BF16)
+        halves = [dot(yv[op, n * (sub // 2):(n + 1) * (sub // 2)], mv[op], 1, 1, HIGHEST) for n in range(2)]
+        for n, x in enumerate(halves):
+            rng = slice(n * (sub // 2), (n + 1) * (sub // 2))
+            xf[op, rng] = x
+            xz[op, z, rng] = x.astype(BF16)
         spread_begin(op)
 
     def rayleigh(op):
@@ -362,7 +364,7 @@
 
     def half_sweep(o_op, t_op, last):
         o, t = ortho(o_op, last), transport(t_op)
-        run("OOTTOTTTOTOOTTOOOOTOTOOO", O=o, T=t)
+        run("OOTTTOTTTTTOTOOTTOOOOTOTOOO", O=o, T=t)
         rest(t)
         rest(o)
 
@@ -385,7 +387,7 @@
     left_basis[...] = xf[0]
     right_basis[...] = xf[1]
     o, t = rayleigh(0), transport(1)
-    run("OOTTOTTTOTO", O=o, T=t)
+    run("OOTTTOTTTTTOTO", O=o, T=t)
     rest(t)
     rest(o)
     rest(rayleigh(1))

time: 374 us -> 368 us (0.984)
  Pallas kernels: 367 us -> 361 us
    pallas_call x1, Pallas kernels: 367 us -> 361 us  [local_program(): pl.pallas_call(functools.partial(kernel, rows, col), out_shape=(basis, ra...]
where the time goes in v6:
time: 368 us
  Pallas kernels  361 us (98%)
  local copies, waits for them, and re-layouts  6.48 us (2%)
    pallas_call x1, Pallas kernels, local_program(): pl.pallas_call(functools.partial(kernel, rows, col), out_shape=(basis, ra...  361 us

profile of v6, /device:TPU:0, one launch (start us, length us, event | category | flops | bytes accessed | tf_op | source)
XLA Modules:
  0.0 367.7 jit_solution(5862061493040727497)
XLA Ops:
  0.6 360.6 %shard_map.75 = (f32[768,128]{1,0:T(8,128)}, f32[128,128]{1,0:T(8,128)}, f32[768,128]{1,0:T(8,128)}, f32[128,128]{1,0:T(8,128)}) custom-call(bf16[3072,3072]{1,0:T(8,128)(2,1)} %left_op.1, f32[768,128]{1,0:T(8,128)} %left_start.1, bf16[3072,3072]{1,0:T(8,128)(2,1)} %right_op.1, f32[768,128]{1,0:T(8,128)} %right_start.1), custom_call_target="tpu_custom_call" | custom-call | tf_op jit(solution)/shard_map/pallas_call | solution.py:433
  361.2 1.8 copy.12
  363.0 1.5 copy.13
  364.4 1.8 copy.14
  366.2 1.5 copy.15
